TPU v7x, 32 devices: a whole 2x2x4 slice. The times are simulated.
32 devices in a mesh: expert: 4 (over y, core), unit: 8 (over z, x).
Axes of the slice: x: 2, y: 2, z: 4, core: 2. Of those that a mesh axis runs over, the one named last changes fastest.
Arguments:
- a_gate: bfloat16 [4, 14336, 4096], P('expert', 'unit'), may hold values from -0.09375 to 0.09375
- a_up: bfloat16 [4, 14336, 4096], P('expert', 'unit'), may hold values from -0.09375 to 0.09375
- b_gate: bfloat16 [4, 14336, 4096], P('expert', 'unit'), may hold values from -0.09375 to 0.09375
- b_up: bfloat16 [4, 14336, 4096], P('expert', 'unit'), may hold values from -0.09375 to 0.09375
- order: int32 [4, 448], P('expert'), may hold values from 0 to 447, each once within a row
- calib: bfloat16 [128, 4096], P(('expert', 'unit')), may hold values from -6 to 6
Outputs:
- merged_gate: bfloat16 [4, 14336, 4096], P('expert', 'unit')
- merged_up: bfloat16 [4, 14336, 4096], P('expert', 'unit')
- hidden: bfloat16 [4, 14336, 128], P('expert', 'unit')
Inputs may be any that keep to these rules, and one draw needn't show every extreme that they name: Each row of order is a permutation of the 448 block numbers.
All inputs are finite; a program needn't handle non-finite values.
Results may differ from a plain program's by a relative error of at most 0.006.
Values may be sent and summed in bfloat16 or wider, within the bound.
A program may use at most 256 MiB of HBM per device.

v0:
```python
import jax
import jax.numpy as jnp
from jax import lax
from jax.sharding import PartitionSpec as P

BLOCK = 32


def average(first, second):
    return ((first.astype(jnp.float32) + second.astype(jnp.float32)) * 0.5).astype(jnp.bfloat16)


def local(a_gate, a_up, b_gate, b_up, order, calib):
    blocks = order.shape[1]
    total = blocks * BLOCK
    inverse = jnp.zeros((blocks,), jnp.int32).at[order[0]].set(jnp.arange(blocks, dtype=jnp.int32))

    def relocate(columns):
        grouped = columns.reshape(blocks, BLOCK, columns.shape[1])
        return jnp.take(grouped, inverse, axis=0).reshape(total, columns.shape[1])

    gathered = (
        lax.all_to_all(b_gate[0], "unit", split_axis=1, concat_axis=0, tiled=True),
        lax.all_to_all(b_up[0], "unit", split_axis=1, concat_axis=0, tiled=True),
    )
    returned = (
        lax.all_to_all(relocate(gathered[0]), "unit", split_axis=0, concat_axis=1, tiled=True),
        lax.all_to_all(relocate(gathered[1]), "unit", split_axis=0, concat_axis=1, tiled=True),
    )
    merged_gate = average(a_gate[0], returned[0])
    merged_up = average(a_up[0], returned[1])
    dims = (((1,), (1,)), ((), ()))
    piece = lax.all_gather(calib, ("expert", "unit"), axis=0, tiled=True)
    gate_pre = lax.dot_general(merged_gate, piece, dims, preferred_element_type=jnp.float32)
    up_pre = lax.dot_general(merged_up, piece, dims, preferred_element_type=jnp.float32)
    hidden = (jax.nn.silu(gate_pre) * up_pre).astype(jnp.bfloat16)
    return (merged_gate[None], merged_up[None], hidden[None])


def solution(mesh):
    in_specs = (
        P("expert", "unit", None),
        P("expert", "unit", None),
        P("expert", "unit", None),
        P("expert", "unit", None),
        P("expert", None),
        P(("expert", "unit"), None),
    )
    out_specs = (P("expert", "unit", None), P("expert", "unit", None), P("expert", "unit", None))
    return jax.shard_map(local, mesh=mesh, in_specs=in_specs, out_specs=out_specs, check_vma=False)
```

profile of v0, /device:TPU:0, one launch (start us, length us, event | category | flops | bytes accessed | tf_op | source)
XLA Modules:
  0.0 1635.2 jit_solution(6001479759196739935)
XLA Ops:
  7.2 18.6 %copy.22 = bf16[1,1792,4096]{1,2,0:T(8,128)(2,1)} copy(bf16[1,1792,4096]{2,1,0:T(8,128)(2,1)} %param.10) | data formatting | bytes 29360128 | tf_op args[2]
  25.8 7.3 all-to-all-start
  33.1 18.6 %copy.26 = bf16[1,1792,4096]{1,2,0:T(8,128)(2,1)} copy(bf16[1,1792,4096]{2,1,0:T(8,128)(2,1)} %param.11) | data formatting | bytes 29360128 | tf_op args[3]
  51.7 299.4 %all-to-all-done = bf16[1792,8,512]{0,2,1:T(8,128)(2,1)} async-done(((bf16[1792,8,512]{0,2,1:T(8,128)(2,1)}), bf16[1792,8,512]{0,2,1:T(8,128)(2,1)}, u32[]{:S(2)}, u32[]{:S(2)}) %all-to-all-start) | async-done | bytes 14680096 | tf_op jit(solution)/shard_map/all_to_all | solution.py:23
  351.1 0.0 copy-start.2
  351.1 5.7 all-to-all-start.2
  356.8 0.0 copy-done.2
  356.8 2.9 scatter_custom_fusion
  359.8 18.7 %copy.23 = bf16[8,1792,512]{2,1,0:T(8,128)(2,1)} copy(bf16[8,1792,512]{1,2,0:T(8,128)(2,1)} %bitcast.3) | data formatting | bytes 29360128 | tf_op jit(solution)/shard_map/all_to_all | solution.py:23
  378.5 295.4 %all-to-all-done.2 = bf16[1792,8,512]{0,2,1:T(8,128)(2,1)} async-done(((bf16[1792,8,512]{0,2,1:T(8,128)(2,1)}), bf16[1792,8,512]{0,2,1:T(8,128)(2,1)}, u32[]{:S(2)}, u32[]{:S(2)}) %all-to-all-start.2) | async-done | bytes 14680096 | tf_op jit(solution)/shard_map/all_to_all | solution.py:24
  673.8 18.7 %copy.27 = bf16[8,1792,512]{2,1,0:T(8,128)(2,1)} copy(bf16[8,1792,512]{1,2,0:T(8,128)(2,1)} %bitcast.9) | data formatting | bytes 29360128 | tf_op jit(solution)/shard_map/all_to_all | solution.py:24
  692.5 18.6 %gather_fusion = bf16[448,32,512]{2,1,0:T(8,128)(2,1)} fusion(bf16[448,32,512]{2,1,0:T(8,128)(2,1)} %bitcast.50, s32[1024]{0:T(1024)S(1)} %pad_clamp_fusion), kind=kCustom, calls=%fused_computation.clone | custom fusion | bytes 29361920 | tf_op jit(solution)/shard_map/jit(_take)/gather | solution.py:20
  711.1 18.6 %gather_fusion.1 = bf16[448,32,512]{2,1,0:T(8,128)(2,1)} fusion(bf16[448,32,512]{2,1,0:T(8,128)(2,1)} %bitcast.52, s32[1024]{0:T(1024)S(1)} %pad_clamp_fusion), kind=kCustom, calls=%fused_computation.1.clone | custom fusion | bytes 29361920 | tf_op jit(solution)/shard_map/jit(_take)/gather | solution.py:20
  729.7 17.3 %broadcast_select_fusion = (bf16[448,32,512]{2,1,0:T(8,128)(2,1)S(1)}, bf16[448,32,512]{2,1,0:T(8,128)(2,1)}) fusion(bf16[448,32,512]{2,1,0:T(8,128)(2,1)} %gather_fusion.1, pred[448]{0:T(512)(128)(4,1)S(1)} %compare_and_fusion, bf16[448,32,512]{2,1,0:T(8,128)(2,1)} %gather_fusion), kind=kLoop, calls=%fused_computation.19 | loop fusion | flops 14680064 | bytes 58720704 | tf_op jit(solution)/shard_map/jit(_take)/select_n | solution.py:20
  747.0 321.5 %all_to_all.58 = bf16[8,1792,512]{2,1,0:T(8,128)(2,1)} all-to-all(bf16[8,1792,512]{2,1,0:T(8,128)(2,1)S(1)} %bitcast.51), channel_id=1, replica_groups=mesh['expert'=4,'unit'=8] {'unit'}, dimensions={0} | all-to-all | bytes 29360128 | tf_op jit(solution)/shard_map/all_to_all | solution.py:28
  1068.5 5.5 all-to-all-start.1
  1074.0 0.2 all-gather.3.cloned.1.call-start
  1074.2 0.5 all-gather.3.cloned.1.call-update
  1074.7 18.6 %copy.21 = bf16[1,1792,4096]{1,2,0:T(8,128)(2,1)} copy(bf16[1,1792,4096]{2,1,0:T(8,128)(2,1)} %param.8) | data formatting | bytes 29360128 | tf_op args[0]
  1093.4 18.8 %copy.25 = bf16[1,1792,4096]{1,2,0:T(8,128)(2,1)} copy(bf16[1,1792,4096]{2,1,0:T(8,128)(2,1)} %param.9) | data formatting | bytes 29360128 | tf_op args[1]
  1112.1 286.1 %all-gather.3.cloned.1.call-done = bf16[32,4,4096]{2,1,0:T(4,128)(2,1)} async-done(((bf16[1,4,4096]{2,1,0:T(4,128)(2,1)}), bf16[32,4,4096]{2,1,0:T(4,128)(2,1)}) %all-gather.3.cloned.1.call-update) | async-done | bytes 1048592 | tf_op jit(solution)/shard_map/all_gather | solution.py:33
  1398.2 1.3 reshape.132
  1399.5 16.8 %convert_bitcast_fusion.2 = f32[1792,8,512]{2,0,1:T(8,128)} fusion(bf16[8,1792,512]{2,1,0:T(8,128)(2,1)} %all_to_all.58), kind=kLoop, calls=%fused_computation.17 | loop fusion | flops 7340032 | bytes 44040192 | tf_op jit(solution)/shard_map/convert_element_type | solution.py:10
  1416.3 27.6 %copy.28 = f32[1792,8,512]{0,2,1:T(8,128)} copy(f32[1792,8,512]{2,0,1:T(8,128)} %convert_bitcast_fusion.2) | data formatting | bytes 58720256 | tf_op jit(solution)/shard_map/convert_element_type | solution.py:10
  1444.0 0.0 copy-start
  1444.0 20.5 %fusion.9 = bf16[1792,4096]{0,1:T(8,128)(2,1)} fusion(bf16[1,1792,4096]{1,2,0:T(8,128)(2,1)} %copy.25, f32[1792,8,512]{0,2,1:T(8,128)} %copy.28), kind=kLoop, calls=%fused_computation.16 | loop fusion | flops 29360128 | bytes 58720256 | tf_op jit(solution)/shard_map/convert_element_type | solution.py:10
  1464.5 6.9 copy-done
  1471.4 14.6 fusion.6
  1486.0 0.0 all-to-all-done.1
  1486.0 16.8 %convert_bitcast_fusion.3 = f32[1792,8,512]{2,0,1:T(8,128)} fusion(bf16[8,1792,512]{2,1,0:T(8,128)(2,1)} %all-to-all-done.1), kind=kLoop, calls=%fused_computation.18 | loop fusion | flops 7340032 | bytes 44040192 | tf_op jit(solution)/shard_map/convert_element_type | solution.py:10
  1502.8 27.6 %copy.24 = f32[1792,8,512]{0,2,1:T(8,128)} copy(f32[1792,8,512]{2,0,1:T(8,128)} %convert_bitcast_fusion.3) | data formatting | bytes 58720256 | tf_op jit(solution)/shard_map/convert_element_type | solution.py:10
  1530.5 0.0 copy-start.1
  1530.5 20.5 %fusion.4 = bf16[1792,4096]{0,1:T(8,128)(2,1)} fusion(bf16[1,1792,4096]{1,2,0:T(8,128)(2,1)} %copy.21, f32[1792,8,512]{0,2,1:T(8,128)} %copy.24), kind=kLoop, calls=%fused_computation.11 | loop fusion | flops 29360128 | bytes 58720256 | tf_op jit(solution)/shard_map/convert_element_type | solution.py:10
  1551.0 6.9 copy-done.1
  1557.9 14.6 fusion.1
  1572.5 20.1 %copy.32 = bf16[1,1792,4096]{2,1,0:T(8,128)(2,1)} copy(bf16[1,1792,4096]{1,2,0:T(8,128)(2,1)} %fusion.6) | data formatting | bytes 29360128
  1592.6 20.1 %copy.31 = bf16[1,1792,4096]{2,1,0:T(8,128)(2,1)} copy(bf16[1,1792,4096]{1,2,0:T(8,128)(2,1)} %fusion.1) | data formatting | bytes 29360128
  1612.7 7.3 fusion.14
  1620.0 8.3 fusion.11
  (5 shorter events, 0.0 us)
Async XLA Ops:
  25.8 325.3 %all-to-all-start = ((bf16[1792,8,512]{0,2,1:T(8,128)(2,1)}), bf16[1792,8,512]{0,2,1:T(8,128)(2,1)}, u32[]{:S(2)}, u32[]{:S(2)}) async-start(bf16[1792,8,512]{0,2,1:T(8,128)(2,1)} %bitcast.48), calls=%async_computation | async-start | bytes 29360128 | tf_op jit(solution)/shard_map/all_to_all | solution.py:23
  351.1 5.7 copy-start.2
  351.1 322.8 %all-to-all-start.2 = ((bf16[1792,8,512]{0,2,1:T(8,128)(2,1)}), bf16[1792,8,512]{0,2,1:T(8,128)(2,1)}, u32[]{:S(2)}, u32[]{:S(2)}) async-start(bf16[1792,8,512]{0,2,1:T(8,128)(2,1)} %bitcast.47), calls=%async_computation.2 | async-start | bytes 29360128 | tf_op jit(solution)/shard_map/all_to_all | solution.py:24
  1068.5 417.6 %all-to-all-start.1 = ((bf16[8,1792,512]{2,1,0:T(8,128)(2,1)}), bf16[8,1792,512]{2,1,0:T(8,128)(2,1)}, u32[]{:S(2)}, u32[]{:S(2)}) async-start(bf16[8,1792,512]{2,1,0:T(8,128)(2,1)} %bitcast.49), calls=%async_computation.1 | async-start | bytes 29360128 | tf_op jit(solution)/shard_map/all_to_all | solution.py:27
  1074.0 324.2 %all-gather.3.cloned.1.call-start = ((), (), s32[]{:S(2)}) async-start(), calls=%async_computation.4 | async-start | bytes 1081344 | tf_op jit(solution)/shard_map/all_gather | solution.py:33
  1444.0 27.5 %copy-start = (f32[1792,8,512]{0,2,1:T(8,128)S(1)}, f32[1792,8,512]{0,2,1:T(8,128)}, u32[]{:S(2)}) copy-start(f32[1792,8,512]{0,2,1:T(8,128)} %copy.28) | copy-start | bytes 88080384
  1530.5 27.5 %copy-start.1 = (f32[1792,8,512]{0,2,1:T(8,128)S(1)}, f32[1792,8,512]{0,2,1:T(8,128)}, u32[]{:S(2)}) copy-start(f32[1792,8,512]{0,2,1:T(8,128)} %copy.24) | copy-start | bytes 88080384
Sparse Core Ops, SparseCore 0:
  1077.8 320.3 all-gather.2
where the time goes:
time: 1640 us
  waiting for transfers between devices  881 us (54%)
  blocking collectives  322 us (20%)
  local copies, waits for them, and re-layouts  263 us (16%)
  other arithmetic  121 us (7%)
  starting transfers between devices  18.7 us (1%)
    all_to_all x1, blocking collectives, local(): lax.all_to_all(relocate(gathered[1]), 'unit', split_axis=0, concat_axis=1...  322 us
    all_to_all x1, waiting for transfers between devices, local(): lax.all_to_all(b_gate[0], 'unit', split_axis=1, concat_axis=0, tiled=True)  299 us
    all_to_all x1, waiting for transfers between devices, local(): lax.all_to_all(b_up[0], 'unit', split_axis=1, concat_axis=0, tiled=True)  295 us
    all_gather x1, waiting for transfers between devices, local(): piece = lax.all_gather(calib, ('expert', 'unit'), axis=0, tiled=True)  286 us
    unnamed x13, local copies, waits for them, and re-layouts  130 us
    convert_element_type x4, other arithmetic, average(): ((first.astype(jnp.float32) + second.astype(jnp.float32)) * 0.5).astype(j...  70.3 us
    convert_element_type x2, local copies, waits for them, and re-layouts, average(): second.astype(jnp.float32)  55.3 us
    gather x2, local copies, waits for them, and re-layouts, relocate(): return jnp.take(grouped, inverse, axis=0).reshape(total, columns.shape[1])  37.1 us
  transfers between devices with their start and end apart: 4, of which 3 were waited for; matrix products, arithmetic and copies ran while one was open for 10% of the time, Pallas kernels for 0%

commit v1 on v0

--- a/solution.py
+++ b/solution.py
@@ -1,9 +1,21 @@
+import functools
 import jax
 import jax.numpy as jnp
 from jax import lax
 from jax.sharding import PartitionSpec as P
 
 BLOCK = 32
+
+
+def _return_all_vectors(x_in, axis_k, where_dim):
+    part_now = lax.axis_size("unit")
+    outcome_arr = jnp.split(x_in, part_now, axis=axis_k)
+    state_now = jnp.stack(outcome_arr)
+    y_new = lax.all_to_all(state_now, "unit", split_axis=0, concat_axis=0)
+    return jnp.concatenate(y_new, axis=where_dim)
+
+
+point_chunk = functools.partial(_return_all_vectors, axis_k=1, where_dim=0)
 
 
 def average(first, second):
@@ -21,7 +33,7 @@
 
     gathered = (
         lax.all_to_all(b_gate[0], "unit", split_axis=1, concat_axis=0, tiled=True),
-        lax.all_to_all(b_up[0], "unit", split_axis=1, concat_axis=0, tiled=True),
+        point_chunk(b_up[0]),
     )
     returned = (
         lax.all_to_all(relocate(gathered[0]), "unit", split_axis=0, concat_axis=1, tiled=True),

time: 1640 us -> 1600 us (0.976)
  waiting for transfers between devices: 881 us -> 859 us
    all_to_all x1 -> x0, local copies, waits for them, and re-layouts: 18.7 us -> none  [local(): lax.all_to_all(b_up[0], 'unit', split_axis=1, concat_axis=0, tiled=True)]
    all_to_all x1, waiting for transfers between devices: 295 us -> 277 us  [_return_all_vectors(): y_new = lax.all_to_all(state_now, 'unit', split_axis=0, concat_axis=0)]
    unnamed x13 -> x19, local copies, waits for them, and re-layouts: 130 us -> 131 us
  transfers between devices with their start and end apart: 4 -> 4, of which waited for: 3 -> 3; matrix products, arithmetic and copies ran while one was open for 10% -> 11% of each run, Pallas kernels for 0% -> 0%
where the time goes in v1:
time: 1600 us
  waiting for transfers between devices  859 us (54%)
  blocking collectives  322 us (20%)
  local copies, waits for them, and re-layouts  248 us (16%)
  other arithmetic  121 us (8%)
  starting transfers between devices  18.6 us (1%)
    all_to_all x1, blocking collectives, local(): lax.all_to_all(relocate(gathered[1]), 'unit', split_axis=0, concat_axis=1...  322 us
    all_to_all x1, waiting for transfers between devices, local(): lax.all_to_all(b_gate[0], 'unit', split_axis=1, concat_axis=0, tiled=True)  295 us
    all_gather x1, waiting for transfers between devices, local(): piece = lax.all_gather(calib, ('expert', 'unit'), axis=0, tiled=True)  286 us
    all_to_all x1, waiting for transfers between devices, _return_all_vectors(): y_new = lax.all_to_all(state_now, 'unit', split_axis=0, concat_axis=0)  277 us
    unnamed x19, local copies, waits for them, and re-layouts  131 us
    convert_element_type x4, other arithmetic, average(): ((first.astype(jnp.float32) + second.astype(jnp.float32)) * 0.5).astype(j...  70.3 us
    convert_element_type x2, local copies, waits for them, and re-layouts, average(): second.astype(jnp.float32)  55.3 us
    gather x2, local copies, waits for them, and re-layouts, relocate(): return jnp.take(grouped, inverse, axis=0).reshape(total, columns.shape[1])  37.1 us
  transfers between devices with their start and end apart: 4, of which 3 were waited for; matrix products, arithmetic and copies ran while one was open for 11% of the time, Pallas kernels for 0%

profile of v1, /device:TPU:0, one launch (start us, length us, event | category | flops | bytes accessed | tf_op | source)
XLA Modules:
  0.0 1597.8 jit_solution(1825311291766361249)
XLA Ops:
  7.2 18.6 %copy.20 = bf16[1,1792,4096]{1,2,0:T(8,128)(2,1)} copy(bf16[1,1792,4096]{2,1,0:T(8,128)(2,1)} %param.10) | data formatting | bytes 29360128 | tf_op args[2]
  25.8 7.3 all-to-all-start
  33.1 2.8 fusion.19
  35.9 2.8 fusion.18
  38.8 2.8 fusion.17
  41.6 2.8 fusion.16
  44.5 2.8 fusion.15
  47.3 2.8 fusion.14
  50.2 2.8 fusion.13
  53.0 2.8 fusion.12
  55.8 0.0 copy-start.2
  55.8 295.2 %all-to-all-done = bf16[1792,8,512]{0,2,1:T(8,128)(2,1)} async-done(((bf16[1792,8,512]{0,2,1:T(8,128)(2,1)}), bf16[1792,8,512]{0,2,1:T(8,128)(2,1)}, u32[]{:S(2)}, u32[]{:S(2)}) %all-to-all-start) | async-done | bytes 14680096 | tf_op jit(solution)/shard_map/all_to_all | solution.py:35
  351.1 5.6 all-to-all-start.2
  356.6 0.0 copy-done.2
  356.7 2.9 scatter_custom_fusion
  359.6 18.7 %copy.21 = bf16[8,1792,512]{2,1,0:T(8,128)(2,1)} copy(bf16[8,1792,512]{1,2,0:T(8,128)(2,1)} %bitcast.3) | data formatting | bytes 29360128 | tf_op jit(solution)/shard_map/all_to_all | solution.py:35
  378.3 18.5 %gather_fusion = bf16[448,32,512]{2,1,0:T(8,128)(2,1)} fusion(bf16[448,32,512]{2,1,0:T(8,128)(2,1)} %bitcast.81, s32[1024]{0:T(1024)S(1)} %pad_clamp_fusion), kind=kCustom, calls=%fused_computation.clone | custom fusion | bytes 29361920 | tf_op jit(solution)/shard_map/jit(_take)/gather | solution.py:32
  396.9 276.9 %all-to-all-done.2 = bf16[8,1792,512]{2,1,0:T(8,128)(2,1)} async-done(((bf16[8,1792,512]{2,1,0:T(8,128)(2,1)}), bf16[8,1792,512]{2,1,0:T(8,128)(2,1)}, u32[]{:S(2)}, u32[]{:S(2)}) %all-to-all-start.2) | async-done | bytes 14680096 | tf_op jit(solution)/shard_map/all_to_all | solution.py:14
  673.7 18.6 %gather_fusion.1 = bf16[448,32,512]{2,1,0:T(8,128)(2,1)} fusion(bf16[448,32,512]{2,1,0:T(8,128)(2,1)} %bitcast.17, s32[1024]{0:T(1024)S(1)} %pad_clamp_fusion), kind=kCustom, calls=%fused_computation.1.clone | custom fusion | bytes 29361920 | tf_op jit(solution)/shard_map/jit(_take)/gather | solution.py:32
  692.3 17.3 %broadcast_select_fusion = (bf16[448,32,512]{2,1,0:T(8,128)(2,1)S(1)}, bf16[448,32,512]{2,1,0:T(8,128)(2,1)}) fusion(bf16[448,32,512]{2,1,0:T(8,128)(2,1)} %gather_fusion.1, pred[448]{0:T(512)(128)(4,1)S(1)} %compare_and_fusion, bf16[448,32,512]{2,1,0:T(8,128)(2,1)} %gather_fusion), kind=kLoop, calls=%fused_computation.19 | loop fusion | flops 14680064 | bytes 58720704 | tf_op jit(solution)/shard_map/jit(_take)/select_n | solution.py:32
  709.6 321.5 %all_to_all.47 = bf16[8,1792,512]{2,1,0:T(8,128)(2,1)} all-to-all(bf16[8,1792,512]{2,1,0:T(8,128)(2,1)S(1)} %bitcast.80), channel_id=1, replica_groups=mesh['expert'=4,'unit'=8] {'unit'}, dimensions={0} | all-to-all | bytes 29360128 | tf_op jit(solution)/shard_map/all_to_all | solution.py:40
  1031.1 5.5 all-to-all-start.1
  1036.6 0.2 all-gather.3.cloned.1.call-start
  1036.8 0.5 all-gather.3.cloned.1.call-update
  1037.4 18.6 %copy.19 = bf16[1,1792,4096]{1,2,0:T(8,128)(2,1)} copy(bf16[1,1792,4096]{2,1,0:T(8,128)(2,1)} %param.8) | data formatting | bytes 29360128 | tf_op args[0]
  1056.0 18.8 %copy.23 = bf16[1,1792,4096]{1,2,0:T(8,128)(2,1)} copy(bf16[1,1792,4096]{2,1,0:T(8,128)(2,1)} %param.9) | data formatting | bytes 29360128 | tf_op args[1]
  1074.8 286.1 %all-gather.3.cloned.1.call-done = bf16[32,4,4096]{2,1,0:T(4,128)(2,1)} async-done(((bf16[1,4,4096]{2,1,0:T(4,128)(2,1)}), bf16[32,4,4096]{2,1,0:T(4,128)(2,1)}) %all-gather.3.cloned.1.call-update) | async-done | bytes 1048592 | tf_op jit(solution)/shard_map/all_gather | solution.py:45
  1360.8 1.3 reshape.123
  1362.2 16.8 %convert_bitcast_fusion.2 = f32[1792,8,512]{2,0,1:T(8,128)} fusion(bf16[8,1792,512]{2,1,0:T(8,128)(2,1)} %all_to_all.47), kind=kLoop, calls=%fused_computation.17 | loop fusion | flops 7340032 | bytes 44040192 | tf_op jit(solution)/shard_map/convert_element_type | solution.py:22
  1379.0 27.6 %copy.24 = f32[1792,8,512]{0,2,1:T(8,128)} copy(f32[1792,8,512]{2,0,1:T(8,128)} %convert_bitcast_fusion.2) | data formatting | bytes 58720256 | tf_op jit(solution)/shard_map/convert_element_type | solution.py:22
  1406.6 0.0 copy-start
  1406.6 20.5 %fusion.9 = bf16[1792,4096]{0,1:T(8,128)(2,1)} fusion(bf16[1,1792,4096]{1,2,0:T(8,128)(2,1)} %copy.23, f32[1792,8,512]{0,2,1:T(8,128)} %copy.24), kind=kLoop, calls=%fused_computation.16 | loop fusion | flops 29360128 | bytes 58720256 | tf_op jit(solution)/shard_map/convert_element_type | solution.py:22
  1427.1 6.9 copy-done
  1434.1 14.6 fusion.6
  1448.7 0.0 all-to-all-done.1
  1448.7 16.8 %convert_bitcast_fusion.3 = f32[1792,8,512]{2,0,1:T(8,128)} fusion(bf16[8,1792,512]{2,1,0:T(8,128)(2,1)} %all-to-all-done.1), kind=kLoop, calls=%fused_computation.18 | loop fusion | flops 7340032 | bytes 44040192 | tf_op jit(solution)/shard_map/convert_element_type | solution.py:22
  1465.4 27.6 %copy.22 = f32[1792,8,512]{0,2,1:T(8,128)} copy(f32[1792,8,512]{2,0,1:T(8,128)} %convert_bitcast_fusion.3) | data formatting | bytes 58720256 | tf_op jit(solution)/shard_map/convert_element_type | solution.py:22
  1493.1 0.0 copy-start.1
  1493.1 20.5 %fusion.4 = bf16[1792,4096]{0,1:T(8,128)(2,1)} fusion(bf16[1,1792,4096]{1,2,0:T(8,128)(2,1)} %copy.19, f32[1792,8,512]{0,2,1:T(8,128)} %copy.22), kind=kLoop, calls=%fused_computation.11 | loop fusion | flops 29360128 | bytes 58720256 | tf_op jit(solution)/shard_map/convert_element_type | solution.py:22
  1513.6 6.9 copy-done.1
  1520.5 14.6 fusion.1
  1535.1 20.1 %copy.28 = bf16[1,1792,4096]{2,1,0:T(8,128)(2,1)} copy(bf16[1,1792,4096]{1,2,0:T(8,128)(2,1)} %fusion.6) | data formatting | bytes 29360128
  1555.2 20.1 %copy.27 = bf16[1,1792,4096]{2,1,0:T(8,128)(2,1)} copy(bf16[1,1792,4096]{1,2,0:T(8,128)(2,1)} %fusion.1) | data formatting | bytes 29360128
  1575.3 7.3 fusion.22
  1582.6 8.3 fusion.11
  (5 shorter events, 0.0 us)
Async XLA Ops:
  25.8 325.3 %all-to-all-start = ((bf16[1792,8,512]{0,2,1:T(8,128)(2,1)}), bf16[1792,8,512]{0,2,1:T(8,128)(2,1)}, u32[]{:S(2)}, u32[]{:S(2)}) async-start(bf16[1792,8,512]{0,2,1:T(8,128)(2,1)} %bitcast.78), calls=%async_computation | async-start | bytes 29360128 | tf_op jit(solution)/shard_map/all_to_all | solution.py:35
  55.8 300.8 %copy-start.2 = (s32[1,448]{1,0:T(1,128)S(1)}, s32[1,448]{1,0:T(1,128)}, u32[]{:S(2)}) copy-start(s32[1,448]{1,0:T(1,128)} %param.12) | copy-start | bytes 5380
  351.1 322.6 %all-to-all-start.2 = ((bf16[8,1792,512]{2,1,0:T(8,128)(2,1)}), bf16[8,1792,512]{2,1,0:T(8,128)(2,1)}, u32[]{:S(2)}, u32[]{:S(2)}) async-start(bf16[8,1792,512]{2,1,0:T(8,128)(2,1)} %fusion.12), calls=%async_computation.2 | async-start | bytes 29360128 | tf_op jit(solution)/shard_map/all_to_all | solution.py:14
  1031.1 417.6 %all-to-all-start.1 = ((bf16[8,1792,512]{2,1,0:T(8,128)(2,1)}), bf16[8,1792,512]{2,1,0:T(8,128)(2,1)}, u32[]{:S(2)}, u32[]{:S(2)}) async-start(bf16[8,1792,512]{2,1,0:T(8,128)(2,1)} %bitcast.79), calls=%async_computation.1 | async-start | bytes 29360128 | tf_op jit(solution)/shard_map/all_to_all | solution.py:39
  1036.6 324.2 %all-gather.3.cloned.1.call-start = ((), (), s32[]{:S(2)}) async-start(), calls=%async_computation.4 | async-start | bytes 1081344 | tf_op jit(solution)/shard_map/all_gather | solution.py:45
  1406.6 27.5 %copy-start = (f32[1792,8,512]{0,2,1:T(8,128)S(1)}, f32[1792,8,512]{0,2,1:T(8,128)}, u32[]{:S(2)}) copy-start(f32[1792,8,512]{0,2,1:T(8,128)} %copy.24) | copy-start | bytes 88080384
  1493.1 27.5 %copy-start.1 = (f32[1792,8,512]{0,2,1:T(8,128)S(1)}, f32[1792,8,512]{0,2,1:T(8,128)}, u32[]{:S(2)}) copy-start(f32[1792,8,512]{0,2,1:T(8,128)} %copy.22) | copy-start | bytes 88080384
Sparse Core Ops, SparseCore 0:
  1040.4 320.3 all-gather.2
